TPU v7x, 32 devices: a whole 2x2x4 slice. The times are simulated.
32 devices in a mesh: gx: 8 (over z, x), gy: 4 (over y, core).
Axes of the slice: x: 2, y: 2, z: 4, core: 2. Of those that a mesh axis runs over, the one named last changes fastest.
Arguments:
- pooled: bfloat16 [4096, 8, 128], P(('gx', 'gy')), may hold values from -6 to 6
- cotangent: bfloat16 [4096, 28, 128], P(('gx', 'gy')), may hold values from -0.09375 to 0.09375
- bilinear: bfloat16 [7, 128, 128], replicated, may hold values from -0.5 to 0.5
- bag_ids: int32 [4096, 8, 4], P(('gx', 'gy')), may hold values from 0 to 8191, as said below
- bag_lens: int32 [4096, 8], P(('gx', 'gy')), may hold values from 1 to 4
- row_home: int32 [8, 8192], replicated, may hold values from 0 to 8191, as said below
Outputs:
- weight_grad: float32 [7, 128, 128], replicated
- table_grad: float32 [8192, 8, 128], P(('gx', 'gy'))
Inputs may be any that keep to these rules, and one draw needn't show every extreme that they name: Each row row_home[f] is a permutation; row r of field f's table is stored at position row_home[f, r] of table_grad's first dimension. Only the first bag_lens entries of a bag are live. The stored position q = row_home[f, bag_ids[sample, f, k]] of an entry lies in the block of 256 positions of device q // 256 (devices in gx+gy order); among all entries of one device's samples, live or not, at most 256 lie in any one device's block; in every device's entries some block is hit exactly 256 times, and one block is hit exactly 256 times by the entries of every device.
All inputs are finite; a program needn't handle non-finite values.
Results may differ from a plain program's by a relative error of at most 0.0035.
Values may be sent and summed in bfloat16 or wider, within the bound.
A program may use at most 64 MiB of HBM per device.

v0:
```python
import jax
import jax.numpy as jnp
from jax import lax
from jax.sharding import PartitionSpec as P

FIELDS = 8
BAG = 4
R_DEV = 256


def pair_list(fields):
    return [(i, j) for i in range(fields) for j in range(i + 1, fields)]


def on_device(pooled, cotangent, bilinear, bag_ids, bag_lens, row_home):
    pair_order = pair_list(FIELDS)
    samples = pooled.shape[0]
    width = pooled.shape[2]
    projected = jnp.einsum(
        "bfd,fde->bfe", pooled[:, : FIELDS - 1], bilinear, preferred_element_type=jnp.float32
    )
    upper_terms = []
    for i in range(FIELDS - 1):
        running = jnp.zeros((samples, width), jnp.float32)
        for p, (a, c) in enumerate(pair_order):
            if a == i:
                running = running + cotangent[:, p].astype(jnp.float32) * pooled[:, c].astype(
                    jnp.float32
                )
        upper_terms.append(running)
    upper_bf = jnp.stack(upper_terms, 1).astype(jnp.bfloat16)
    local_weight = jnp.einsum(
        "bfd,bfe->fde", pooled[:, : FIELDS - 1], upper_bf, preferred_element_type=jnp.float32
    )
    weight_grad = lax.psum(local_weight, ("gx", "gy"))
    back_terms = jnp.einsum("bfe,fde->bfd", upper_bf, bilinear, preferred_element_type=jnp.float32)
    field_list = []
    for i in range(FIELDS):
        running = back_terms[:, i] if i < FIELDS - 1 else jnp.zeros((samples, width), jnp.float32)
        for p, (a, c) in enumerate(pair_order):
            if c == i:
                running = running + cotangent[:, p].astype(jnp.float32) * projected[:, a]
        field_list.append(running)
    field_grads = jnp.stack(field_list, 1).astype(jnp.bfloat16)
    size_gx = lax.axis_size("gx")
    size_gy = lax.axis_size("gy")
    owners_all = size_gx * size_gy
    entries = samples * FIELDS * BAG
    capacity = max(1, 2 * entries // owners_all)
    sentinel = R_DEV * FIELDS
    field_index = jnp.arange(FIELDS, dtype=jnp.int32)[None, :, None]
    stored = row_home[field_index, bag_ids]
    live = jnp.arange(BAG, dtype=jnp.int32)[None, None, :] < bag_lens[:, :, None]
    owner = (stored // R_DEV).reshape(-1)
    target = jnp.where(live, stored % R_DEV * FIELDS + field_index, sentinel).reshape(-1)
    values = jnp.where(live[:, :, :, None], field_grads[:, :, None, :], jnp.zeros((), jnp.bfloat16))
    values = values.reshape(entries, width)
    block_rows = 128
    blocks = entries // block_rows
    owner_ids = jnp.arange(owners_all, dtype=jnp.int32)
    owner_table = (owner.reshape(blocks, block_rows, 1) == owner_ids[None, None, :]).astype(
        jnp.bfloat16
    )
    row_pos = jnp.arange(block_rows, dtype=jnp.int32)
    earlier = (row_pos[:, None] > row_pos[None, :]).astype(jnp.bfloat16)
    within_all = jnp.einsum("ij,bjo->bio", earlier, owner_table, preferred_element_type=jnp.float32)
    block_totals = jnp.sum(owner_table.astype(jnp.float32), axis=1)
    block_start = jnp.cumsum(block_totals, axis=0) - block_totals
    ahead = within_all + block_start[:, None, :]
    rank = jnp.sum(ahead * owner_table.astype(jnp.float32), axis=2).reshape(-1).astype(jnp.int32)
    place = owner * capacity + rank
    send_values = (
        jnp.zeros((owners_all * capacity, width), jnp.bfloat16)
        .at[place]
        .set(values, unique_indices=True)
    )
    send_target = (
        jnp.full((owners_all * capacity,), sentinel, jnp.int32)
        .at[place]
        .set(target, unique_indices=True)
    )
    send_values = send_values.reshape(size_gx, size_gy, capacity, width)
    send_target = send_target.reshape(size_gx, size_gy, capacity)
    got_values, got_target = (
        lax.all_to_all(
            lax.all_to_all(send_values, "gy", split_axis=1, concat_axis=1, tiled=True),
            "gx",
            split_axis=0,
            concat_axis=0,
            tiled=True,
        ),
        lax.all_to_all(
            lax.all_to_all(send_target, "gy", split_axis=1, concat_axis=1, tiled=True),
            "gx",
            split_axis=0,
            concat_axis=0,
            tiled=True,
        ),
    )
    summed = jax.ops.segment_sum(
        got_values.reshape(-1, width).astype(jnp.float32),
        got_target.reshape(-1),
        num_segments=sentinel + 1,
    )
    table_grad = summed[:sentinel].reshape(R_DEV, FIELDS, width)
    return (weight_grad, table_grad)


def solution(mesh):
    placed = (
        P(("gx", "gy"), None, None),
        P(("gx", "gy"), None, None),
        P(),
        P(("gx", "gy"), None, None),
        P(("gx", "gy"), None),
        P(),
    )
    return jax.shard_map(
        on_device,
        mesh=mesh,
        in_specs=placed,
        out_specs=(P(), P(("gx", "gy"), None, None)),
        check_vma=False,
    )
```

profile of v0, /device:TPU:0, one launch (start us, length us, event | category | flops | bytes accessed | tf_op | source)
XLA Modules:
  0.0 337.1 jit_solution(13678758075913814048)
XLA Ops:
  7.2 0.8 fusion.102
  8.0 0.3 copy.219
  8.2 0.3 reshape.231
  8.5 25.5 %gather_fusion = s32[4096]{0:T(1024)S(1)} fusion(s32[8,8192]{1,0:T(8,128)S(1)} %copy-done, s32[4096]{0:T(1024)S(1)} %reshape.231), kind=kCustom, calls=%fused_computation | custom fusion | bytes 65536 | tf_op jit(solution)/shard_map/gather | solution.py:52
  34.0 0.2 convert_reduce_fusion
  34.3 0.3 fusion.4
  34.7 0.2 iota_compare_fusion
  34.9 0.3 lt.51
  35.3 0.3 add.296
  35.7 15.5 %scatter_custom_fusion = s32[8192]{0:T(1024)S(1)} fusion(s32[4096]{0:T(1024)S(1)} %bitcast.64, s32[4096]{0:T(1024)S(1)} %fusion.98, s32[]{:T(128)} %constant.25.clone.1), kind=kCustom, calls=%fused_computation.188 | custom fusion | bytes 32772 | tf_op jit(solution)/shard_map/scatter | solution.py:80
  51.3 0.6 copy.221
  51.9 4.3 %all-to-all-start = ((s32[8,4,256]{2,0,1:T(8,128)}), s32[8,4,256]{2,0,1:T(8,128)S(1)}, u32[]{:S(2)}, u32[]{:S(2)}) async-start(s32[8,4,256]{2,0,1:T(8,128)} %copy.221), calls=%async_computation | async-start | bytes 65536 | tf_op jit(solution)/shard_map/all_to_all | solution.py:93
  56.3 0.4 fusion.109
  56.8 0.1 copy.244
  56.9 0.1 copy.242
  57.1 0.1 copy.240
  57.2 0.1 copy.233
  57.4 0.1 copy.237
  57.6 0.1 copy.239
  57.7 0.1 copy.241
  57.8 0.1 copy.243
  57.9 0.1 copy.245
  58.1 0.1 copy.238
  58.2 0.1 copy.236
  58.3 0.1 copy.234
  58.5 0.1 copy.249
  58.6 0.1 copy.250
  58.7 0.1 copy.251
  58.8 0.1 copy.252
  59.0 0.1 copy.247
  59.1 0.1 copy.248
  59.2 0.1 copy.253
  59.3 0.1 copy.254
  59.5 0.1 copy.255
  59.6 0.1 copy.256
  59.7 0.1 copy.257
  59.8 0.1 copy.258
  60.0 0.1 copy.259
  60.1 0.1 copy.260
  60.2 0.1 copy.261
  60.3 0.1 copy.262
  60.5 0.1 copy.263
  60.7 0.1 copy.265
  61.0 0.1 copy.267
  61.5 0.2 convolution_bitcast_fusion
  61.7 0.4 copy-done.3
  62.2 0.3 convolution_bitcast_fusion.1
  62.9 0.2 copy.226
  63.1 0.4 broadcast_in_dim.61
  63.4 13.8 %scatter_custom_fusion.1 = bf16[8192,128]{1,0:T(8,128)(2,1)S(1)} fusion(s32[4096]{0:T(1024)S(1)} %bitcast.65, bf16[4096,128]{1,0:T(8,128)(2,1)S(1)} %bitcast.58, bf16[]{:T(256)} %constant.49.clone.1, pred[4096]{0:T(1024)(128)(4,1)S(1)} %lt.51), kind=kCustom, calls=%fused_computation.14 | custom fusion | flops 524288 | bytes 3150848 | tf_op jit(solution)/shard_map/scatter | solution.py:75
  77.2 1.5 copy.227
  78.7 3.6 %all-to-all-start.2 = ((bf16[8,4,256,128]{3,2,0,1:T(8,128)(2,1)}), bf16[8,4,256,128]{3,2,0,1:T(8,128)(2,1)S(1)}, u32[]{:S(2)}, u32[]{:S(2)}) async-start(bf16[8,4,256,128]{3,2,0,1:T(8,128)(2,1)} %copy.227), calls=%async_computation.2 | async-start | bytes 4194304 | tf_op jit(solution)/shard_map/all_to_all | solution.py:86
  82.3 0.6 copy.222
  82.9 25.0 %all-to-all-done.2 = bf16[8,4,256,128]{3,2,0,1:T(8,128)(2,1)S(1)} async-done(((bf16[8,4,256,128]{3,2,0,1:T(8,128)(2,1)}), bf16[8,4,256,128]{3,2,0,1:T(8,128)(2,1)S(1)}, u32[]{:S(2)}, u32[]{:S(2)}) %all-to-all-start.2) | async-done | bytes 2097184 | tf_op jit(solution)/shard_map/all_to_all | solution.py:86
  107.9 6.3 %all-to-all-start.1 = ((s32[8,4,256]{2,1,0:T(4,128)}), s32[8,4,256]{2,1,0:T(4,128)S(1)}, u32[]{:S(2)}, u32[]{:S(2)}) async-start(s32[8,4,256]{2,1,0:T(4,128)} %copy.222), calls=%async_computation.1 | async-start | bytes 65536 | tf_op jit(solution)/shard_map/all_to_all | solution.py:92
  114.2 1.5 copy.228
  115.7 5.2 %all-to-all-done.1 = s32[8,4,256]{2,1,0:T(4,128)S(1)} async-done(((s32[8,4,256]{2,1,0:T(4,128)}), s32[8,4,256]{2,1,0:T(4,128)S(1)}, u32[]{:S(2)}, u32[]{:S(2)}) %all-to-all-start.1) | async-done | bytes 32800 | tf_op jit(solution)/shard_map/all_to_all | solution.py:92
  120.9 3.6 %all-to-all-start.3 = ((bf16[8,4,256,128]{3,2,1,0:T(8,128)(2,1)}), bf16[8,4,256,128]{3,2,1,0:T(8,128)(2,1)S(1)}, u32[]{:S(2)}, u32[]{:S(2)}) async-start(bf16[8,4,256,128]{3,2,1,0:T(8,128)(2,1)} %copy.228), calls=%async_computation.3 | async-start | bytes 4194304 | tf_op jit(solution)/shard_map/all_to_all | solution.py:85
  124.5 0.2 all-reduce.2.cloned.1.call-start
  124.8 1.0 convolution_bitcast_fusion.2
  125.8 147.7 %all-reduce.2.cloned.1.call-done = f32[7,128,128]{1,2,0:T(8,128)} async-done(((f32[7,128,128]{1,2,0:T(8,128)}), f32[7,128,128]{1,2,0:T(8,128)}) %all-reduce.2.cloned.1.call-update) | async-done | bytes 458768 | tf_op jit(solution)/shard_map/psum | solution.py:35
  273.5 2.0 copy.229
  275.5 53.7 %scatter_custom_fusion.2 = f32[2049,128]{1,0:T(8,128)S(1)} fusion(s32[8192]{0:T(1024)S(1)} %bitcast.63, bf16[8192,128]{1,0:T(8,128)(2,1)S(1)} %bitcast.56, f32[]{:T(128)} %constant.21.clone.1), kind=kCustom, calls=%fused_computation.4 | custom fusion | flops 2097152 | bytes 3146244 | tf_op jit(solution)/shard_map/scatter-add | solution.py:100
  329.2 1.0 slice_bitcast_fusion
  (49 shorter events, 1.7 us)
Async XLA Ops:
  7.2 1.3 copy-start
  8.5 26.1 %copy-start.7 = (s32[128,8]{0,1:T(8,128)S(1)}, s32[128,8]{0,1:T(8,128)}, u32[]{:S(2)}) copy-start(s32[128,8]{0,1:T(8,128)} %param.10) | copy-start | bytes 12292
  34.0 22.2 %copy-start.6 = (bf16[128,28,128]{2,0,1:T(8,128)(2,1)S(1)}, bf16[128,28,128]{2,0,1:T(8,128)(2,1)}, u32[]{:S(2)}) copy-start(bf16[128,28,128]{2,0,1:T(8,128)(2,1)} %param.7) | copy-start | bytes 2752516
  34.3 22.0 %copy-start.1 = (bf16[128,8,128]{2,1,0:T(8,128)(2,1)S(1)}, bf16[128,8,128]{2,1,0:T(8,128)(2,1)}, u32[]{:S(2)}) copy-start(bf16[128,8,128]{2,1,0:T(8,128)(2,1)} %param.6) | copy-start | bytes 786436
  51.9 26.8 %all-to-all-start = ((s32[8,4,256]{2,0,1:T(8,128)}), s32[8,4,256]{2,0,1:T(8,128)S(1)}, u32[]{:S(2)}, u32[]{:S(2)}) async-start(s32[8,4,256]{2,0,1:T(8,128)} %copy.221), calls=%async_computation | async-start | bytes 65536 | tf_op jit(solution)/shard_map/all_to_all | solution.py:93
  57.3 4.2 %copy-start.5 = (bf16[7,128,128]{2,1,0:T(8,128)(2,1)S(1)}, bf16[7,128,128]{2,1,0:T(8,128)(2,1)}, u32[]{:S(2)}) copy-start(bf16[7,128,128]{2,1,0:T(8,128)(2,1)} %param.8) | copy-start | bytes 688132
  61.5 0.7 copy-start.3
  78.7 29.2 %all-to-all-start.2 = ((bf16[8,4,256,128]{3,2,0,1:T(8,128)(2,1)}), bf16[8,4,256,128]{3,2,0,1:T(8,128)(2,1)S(1)}, u32[]{:S(2)}, u32[]{:S(2)}) async-start(bf16[8,4,256,128]{3,2,0,1:T(8,128)(2,1)} %copy.227), calls=%async_computation.2 | async-start | bytes 4194304 | tf_op jit(solution)/shard_map/all_to_all | solution.py:86
  107.9 13.0 %all-to-all-start.1 = ((s32[8,4,256]{2,1,0:T(4,128)}), s32[8,4,256]{2,1,0:T(4,128)S(1)}, u32[]{:S(2)}, u32[]{:S(2)}) async-start(s32[8,4,256]{2,1,0:T(4,128)} %copy.222), calls=%async_computation.1 | async-start | bytes 65536 | tf_op jit(solution)/shard_map/all_to_all | solution.py:92
  115.7 9.1 %copy-start.2 = (bf16[128,8,128]{2,1,0:T(8,128)(2,1)S(1)}, bf16[128,8,128]{2,1,0:T(8,128)(2,1)}, u32[]{:S(2)}) copy-start(bf16[128,8,128]{2,1,0:T(8,128)(2,1)} %param.6) | copy-start | bytes 786436
  115.7 9.1 %copy-start.4 = (bf16[128,7,128]{0,2,1:T(8,128)(2,1)S(1)}, bf16[128,7,128]{0,2,1:T(8,128)(2,1)}, u32[]{:S(2)}) copy-start(bf16[128,7,128]{0,2,1:T(8,128)(2,1)} %copy-done.3) | copy-start | bytes 688132
  120.9 154.6 %all-to-all-start.3 = ((bf16[8,4,256,128]{3,2,1,0:T(8,128)(2,1)}), bf16[8,4,256,128]{3,2,1,0:T(8,128)(2,1)S(1)}, u32[]{:S(2)}, u32[]{:S(2)}) async-start(bf16[8,4,256,128]{3,2,1,0:T(8,128)(2,1)} %copy.228), calls=%async_computation.3 | async-start | bytes 4194304 | tf_op jit(solution)/shard_map/all_to_all | solution.py:85
  124.5 149.0 %all-reduce.2.cloned.1.call-start = ((), (), s32[]{:S(2)}) async-start(), calls=%async_computation.4 | async-start | bytes 917504 | tf_op jit(solution)/shard_map/psum | solution.py:35
Sparse Core Ops, SparseCore 0:
  131.2 142.2 all-reduce.1
where the time goes:
time: 341 us; the launch traced here: 337 us
  waiting for transfers between devices  178 us (52%)
  other arithmetic  69.5 us (20%)
  local copies, waits for them, and re-layouts  55.3 us (16%)
  starting transfers between devices  18 us (5%)
  between operations  14.5 us (4%)
    psum x1, waiting for transfers between devices, on_device(): weight_grad = lax.psum(local_weight, ('gx', 'gy'))  148 us
    scatter-add x1, other arithmetic, on_device(): jax.ops.segment_sum(got_values.reshape(-1, width).astype(jnp.float32), go...  53.7 us
    gather x1, local copies, waits for them, and re-layouts, on_device(): stored = row_home[field_index, bag_ids]  25.5 us
    all_to_all x1, waiting for transfers between devices, on_device(): lax.all_to_all(send_values, 'gy', split_axis=1, concat_axis=1, tiled=True)  25 us
    scatter x1, local copies, waits for them, and re-layouts, on_device(): send_target = jnp.full((owners_all * capacity,), sentinel, jnp.int32).at[...  15.5 us
    scatter x1, other arithmetic, on_device(): send_values = jnp.zeros((owners_all * capacity, width), jnp.bfloat16).at[...  13.8 us
  transfers between devices with their start and end apart: 5, of which 3 were waited for; matrix products, arithmetic and copies ran while one was open for 8% of the time, Pallas kernels for 0%

commit v1 on v0

v1 whole, which is shorter than its diff:
```python
import functools

import jax
import jax.numpy as jnp
from jax import lax
from jax.experimental import pallas as pl
from jax.experimental.pallas import tpu as pltpu
from jax.sharding import PartitionSpec as P

MESH = pl.DeviceIdType.MESH
BF = jnp.bfloat16
F32 = jnp.float32
LANES = 128


def pair_list(fields):
    return [(i, j) for i in range(fields) for j in range(i + 1, fields)]


def local_kernel(
    pooled_ref, cot_ref, bil_ref, bag_ref, lens_ref, home_ref,
    grad_ref, weight_ref, ids_ref, pool_f, cot_f, proj_f,
):
    samples, fields, width = pooled_ref.shape
    pairs = cot_ref.shape[1]
    stride = cot_f.shape[0] // samples
    bag = bag_ref.shape[0]

    def spread(b, carry):
        pool_f[pl.ds(pl.multiple_of(b * fields, fields), fields), :] = pooled_ref[b].astype(F32)
        cot_f[pl.ds(pl.multiple_of(b * stride, stride), pairs), :] = cot_ref[b].astype(F32)
        return carry

    lax.fori_loop(0, samples, spread, 0, unroll=8)

    high = [bag_ref[k] // LANES for k in range(bag)]
    low = [bag_ref[k] % LANES for k in range(bag)]

    def look(h, found):
        row = home_ref[:, pl.ds(pl.multiple_of(h * LANES, LANES), LANES)]
        return tuple(
            jnp.where(high[k] == h, jnp.take_along_axis(row, low[k], axis=1), found[k])
            for k in range(bag)
        )

    none = jnp.full(bag_ref.shape[1:], -1, jnp.int32)
    found = lax.fori_loop(0, home_ref.shape[1] // LANES, look, (none,) * bag, unroll=8)
    lens = lens_ref[...]
    for k in range(bag):
        ids_ref[k] = jnp.where(lens > k, found[k], -1)

    pool = lambda f: pool_f[pl.ds(f, samples, stride=fields), :]
    cot = lambda p: cot_f[pl.ds(p, samples, stride=stride), :]
    number = {pair: p for p, pair in enumerate(pair_list(fields))}
    for i in range(fields - 1):
        proj_f[i] = jnp.dot(pool(i).astype(BF), bil_ref[i], preferred_element_type=F32)
    for i in range(fields):
        total = jnp.zeros((samples, width), F32)
        if i < fields - 1:
            upper = jnp.zeros((samples, width), F32)
            for j in range(i + 1, fields):
                upper = upper + cot(number[i, j]) * pool(j)
            upper = upper.astype(BF)
            weight_ref[i] = lax.dot_general(
                pool(i).astype(BF), upper, (((0,), (0,)), ((), ())), preferred_element_type=F32
            ).astype(BF)
            total = lax.dot_general(
                upper, bil_ref[i], (((1,), (1,)), ((), ())), preferred_element_type=F32
            )
        for k in range(i):
            total = total + cot(number[k, i]) * proj_f[k]
        grad_ref[i] = total.astype(BF)


def exchange_kernel(
    size_gx, size_gy,
    grad_ref, ids_ref, w_ref, out_ref, wout_ref,
    gath, idg, part, got, w1, w2, w2s, w3, w3s,
    zs, zr, ss, sr, ps, pr, w1s_sem, w1r_sem, w2s_sem, w2r_sem, w3s_sem, w3r_sem,
):
    fields, samples, width = grad_ref.shape
    bag = ids_ref.shape[0]
    rows = part.shape[2]
    nz, ny = size_gx // 2, size_gy // 2
    npc, plane = 2 * ny, 2 * size_gy
    gx, gy = lax.axis_index("gx"), lax.axis_index("gy")
    z, x, y, c = gx // 2, gx % 2, gy // 2, gy % 2
    spot = x * ny + y
    seat = x * size_gy + gy
    sibling = (gx, y * 2 + 1 - c)

    def z_peer(d):
        return (((z + d) % nz) * 2 + x, gy)

    def spot_peer(d):
        to = (spot + d) % npc
        return (z * 2 + to // ny, (to % ny) * 2 + c)

    def seat_peer(d):
        to = (seat + d) % plane
        return (z * 2 + to // size_gy, to % size_gy)

    def remote(src, dst, send, recv, dev):
        return pltpu.make_async_remote_copy(
            src_ref=src, dst_ref=dst, send_sem=send, recv_sem=recv,
            device_id=dev, device_id_type=MESH,
        )

    def z_copy(f, d):
        return remote(grad_ref.at[f], gath.at[f, d], zs.at[f * nz + d], zr.at[f * nz + d], z_peer(d))

    def z_ids(d):
        return remote(ids_ref, idg.at[d], zs.at[fields * nz + d], zr.at[fields * nz + d], z_peer(d))

    def s_copy(f, d):
        src = grad_ref.at[f] if d == 0 else gath.at[f, d]
        return remote(src, gath.at[f, nz + d], ss.at[f * nz + d], sr.at[f * nz + d], sibling)

    def s_ids(d):
        src = ids_ref if d == 0 else idg.at[d]
        return remote(src, idg.at[nz + d], ss.at[fields * nz + d], sr.at[fields * nz + d], sibling)

    def p_copy(f, d):
        return remote(part.at[d, f], got.at[d, f], ps.at[f * npc + d], pr.at[f * npc + d], spot_peer(d))

    def w1_copy(d):
        return remote(
            w_ref.at[(seat + d) % plane], w1.at[d], w1s_sem.at[d], w1r_sem.at[d], seat_peer(d)
        )

    def w2_copy(d, slot):
        return remote(w2s, w2.at[slot], w2s_sem.at[d], w2r_sem.at[slot], z_peer(d))

    def w3_copy(d, slot):
        return remote(w3s, w3.at[slot], w3s_sem.at[d], w3r_sem.at[slot], seat_peer(d))

    barrier = pltpu.get_barrier_semaphore()
    for d in range(1, nz):
        pl.semaphore_signal(barrier, inc=1, device_id=z_peer(d), device_id_type=MESH)
    for d in range(1, plane):
        pl.semaphore_signal(barrier, inc=1, device_id=seat_peer(d), device_id_type=MESH)
    pl.semaphore_wait(barrier, nz - 1 + plane - 1)

    for d in range(1, nz):
        z_ids(d).start()
    s_ids(0).start()

    def launch(f, carry):
        for d in range(1, nz):
            z_copy(f, d).start()
        s_copy(f, 0).start()
        return carry

    lax.fori_loop(0, fields, launch, 0)
    for d in range(1, plane):
        w1_copy(d).start()
    gath[:, 0] = grad_ref[...]
    idg[0] = ids_ref[...]

    def forward(f):
        for d in range(1, nz):
            z_copy(f, d).wait_recv()
            s_copy(f, d).start()

    for d in range(1, nz):
        z_ids(d).wait_recv()
        s_ids(d).start()
    forward(0)
    for d in range(nz):
        s_ids(d).wait_recv()

    kind = BF if rows <= 256 else F32
    row_number = lax.broadcasted_iota(jnp.int32, (rows, samples), 0).astype(F32).astype(kind)
    one, zero = jnp.ones((), kind), jnp.zeros((), kind)

    def sums_for(f, d):
        gx_to, gy_to = spot_peer(d)
        base = (gx_to * size_gy + gy_to) * rows
        blocks = []
        for j in range(2 * nz):
            count = None
            for k in range(bag):
                rel = idg[j, k, pl.ds(f, 1), :] - base
                rel = jnp.where((rel >= 0) & (rel < rows), rel, rows).astype(F32).astype(kind)
                hit = jnp.where(row_number == rel, one, zero)
                count = hit if count is None else count + hit
            blocks.append(count.astype(BF))
        return jnp.dot(
            jnp.concatenate(blocks, axis=1),
            gath[f].reshape(2 * nz * samples, width),
            preferred_element_type=F32,
        )

    def weights_in_plane():
        total = w_ref[seat].astype(F32)
        for d in range(1, plane):
            w1_copy(d).wait_recv()
            total = total + w1[d].astype(F32)
        w2s[...] = total.astype(BF)
        w2[z] = total.astype(BF)
        for d in range(1, nz):
            w2_copy(d, z).start()

    def weights_along_z():
        for d in range(1, nz):
            w2_copy(d, (z + d) % nz).wait_recv()
        total = w2[0].astype(F32)
        for s in range(1, nz):
            total = total + w2[s].astype(F32)
        w3s[...] = total.astype(BF)
        w3[seat] = total.astype(BF)
        for d in range(1, plane):
            w3_copy(d, seat).start()

    def one_field(f, carry):
        @pl.when(f + 1 < fields)
        def _():
            forward(f + 1)

        for d in range(nz):
            s_copy(f, d).wait_recv()

        def one_target(d, inner):
            part[d, f] = sums_for(f, d).astype(BF)
            p_copy(f, d).start()
            return inner

        lax.fori_loop(1, npc, one_target, 0)
        out_ref[pl.ds(f, rows, stride=fields), :] = sums_for(f, 0)

        @pl.when(f == 1)
        def _():
            weights_in_plane()

        @pl.when(f == 4)
        def _():
            weights_along_z()

        return carry

    lax.fori_loop(0, fields, one_field, 0)

    for d in range(1, plane):
        w3_copy(d, (seat + d) % plane).wait_recv()
    wout_ref[...] = w3[...].astype(F32)

    def finish(f, carry):
        at = pl.ds(f, rows, stride=fields)
        total = out_ref[at, :]
        for d in range(1, npc):
            p_copy(f, d).wait_recv()
            total = total + got[d, f].astype(F32)
        out_ref[at, :] = total
        return carry

    lax.fori_loop(0, fields, finish, 0)

    def drain(f, carry):
        for d in range(1, nz):
            z_copy(f, d).wait_send()
        for d in range(nz):
            s_copy(f, d).wait_send()
        for d in range(1, npc):
            p_copy(f, d).wait_send()
        return carry

    lax.fori_loop(0, fields, drain, 0)
    for d in range(1, nz):
        z_ids(d).wait_send()
        w2_copy(d, z).wait_send()
    for d in range(nz):
        s_ids(d).wait_send()
    for d in range(1, plane):
        w1_copy(d).wait_send()
        w3_copy(d, seat).wait_send()


def on_device(size_gx, size_gy, pooled, cotangent, bilinear, bag_ids, bag_lens, row_home):
    samples, fields, width = pooled.shape
    bag = bag_ids.shape[2]
    pairs = cotangent.shape[1]
    devices = size_gx * size_gy
    rows = row_home.shape[1] // devices
    nz, npc, plane = size_gx // 2, size_gy, 2 * size_gy
    stride = -(-pairs // 8) * 8
    vmem = pl.BlockSpec(memory_space=pltpu.VMEM)
    grads, weights, ids = pl.pallas_call(
        local_kernel,
        out_shape=(
            jax.ShapeDtypeStruct((fields, samples, width), BF),
            jax.ShapeDtypeStruct((fields - 1, width, width), BF),
            jax.ShapeDtypeStruct((bag, fields, samples), jnp.int32),
        ),
        in_specs=[vmem] * 6,
        out_specs=(vmem,) * 3,
        scratch_shapes=[
            pltpu.VMEM((samples * fields, width), F32),
            pltpu.VMEM((samples * stride, width), F32),
            pltpu.VMEM((fields - 1, samples, width), F32),
        ],
    )(
        pooled, cotangent, bilinear,
        bag_ids.transpose(2, 1, 0), bag_lens.transpose(1, 0), row_home,
    )
    piece = (fields - 1) * width // plane
    dma = pltpu.SemaphoreType.DMA
    table, weight = pl.pallas_call(
        functools.partial(exchange_kernel, size_gx, size_gy),
        out_shape=(
            jax.ShapeDtypeStruct((rows * fields, width), F32),
            jax.ShapeDtypeStruct((plane, piece, width), F32),
        ),
        in_specs=[vmem] * 3,
        out_specs=(vmem,) * 2,
        scratch_shapes=[
            pltpu.VMEM((fields, 2 * nz, samples, width), BF),
            pltpu.VMEM((2 * nz, bag, fields, samples), jnp.int32),
            pltpu.VMEM((npc, fields, rows, width), BF),
            pltpu.VMEM((npc, fields, rows, width), BF),
            pltpu.VMEM((plane, piece, width), BF),
            pltpu.VMEM((nz, piece, width), BF),
            pltpu.VMEM((piece, width), BF),
            pltpu.VMEM((plane, piece, width), BF),
            pltpu.VMEM((piece, width), BF),
            dma(((fields + 1) * nz,)),
            dma(((fields + 1) * nz,)),
            dma(((fields + 1) * nz,)),
            dma(((fields + 1) * nz,)),
            dma((fields * npc,)),
            dma((fields * npc,)),
            dma((plane,)),
            dma((plane,)),
            dma((nz,)),
            dma((nz,)),
            dma((plane,)),
            dma((plane,)),
        ],
        compiler_params=pltpu.CompilerParams(collective_id=0, has_side_effects=True),
    )(grads, ids, weights.reshape(plane, piece, width))
    return (
        weight.reshape(fields - 1, width, width),
        table.reshape(rows, fields, width),
    )


def solution(mesh):
    placed = (
        P(("gx", "gy"), None, None),
        P(("gx", "gy"), None, None),
        P(),
        P(("gx", "gy"), None, None),
        P(("gx", "gy"), None),
        P(),
    )
    return jax.shard_map(
        functools.partial(on_device, mesh.shape["gx"], mesh.shape["gy"]),
        mesh=mesh,
        in_specs=placed,
        out_specs=(P(), P(("gx", "gy"), None, None)),
        check_vma=False,
    )
```

time: 341 us -> 66.2 us (0.19); the launches traced: 337 us -> 65.9 us
  waiting for transfers between devices: 178 us -> 0 us
  other arithmetic: 69.5 us -> 0 us
  Pallas kernels: 0 us -> 57.1 us
  local copies, waits for them, and re-layouts: 55.3 us -> 8.15 us
  starting transfers between devices: 18 us -> 0 us
  between operations: 14.5 us -> 0.64 us
    psum x1 -> x0, waiting for transfers between devices: 148 us -> none  [on_device(): weight_grad = lax.psum(local_weight, ('gx', 'gy'))]
    pallas_call x0 -> x2, Pallas kernels: none -> 57.1 us  [the longest x1 51.2 us: on_device(): pl.pallas_call(functools.partial(exchange_kernel, size_gx, size_gy), out_...]
    scatter-add x1 -> x0, other arithmetic: 53.7 us -> none  [on_device(): jax.ops.segment_sum(got_values.reshape(-1, width).astype(jnp.float32), go...]
    all_to_all x4 -> x0, waiting for transfers between devices: 30.2 us -> none  [the longest x1 25 us: on_device(): lax.all_to_all(send_values, 'gy', split_axis=1, concat_axis=1, tiled=True)]
    gather x1 -> x0, local copies, waits for them, and re-layouts: 25.5 us -> none  [on_device(): stored = row_home[field_index, bag_ids]]
    all_to_all x4 -> x0, starting transfers between devices: 17.8 us -> none  [the longest x1 6.3 us: on_device(): lax.all_to_all(lax.all_to_all(send_target, 'gy', split_axis=1, concat_axi...]
    scatter x1 -> x0, local copies, waits for them, and re-layouts: 15.5 us -> none  [on_device(): send_target = jnp.full((owners_all * capacity,), sentinel, jnp.int32).at[...]
    scatter x1 -> x0, other arithmetic: 13.8 us -> none  [on_device(): send_values = jnp.zeros((owners_all * capacity, width), jnp.bfloat16).at[...]
  transfers between devices with their start and end apart: 5 -> 0, of which waited for: 3 -> 0; matrix products, arithmetic and copies ran while one was open for 8% -> 0% of each run, Pallas kernels for 0% -> 0%
where the time goes in v1:
time: 66.2 us; the launch traced here: 65.9 us
  Pallas kernels  57.1 us (86%)
  local copies, waits for them, and re-layouts  8.15 us (12%)
    pallas_call x1, Pallas kernels, on_device(): pl.pallas_call(functools.partial(exchange_kernel, size_gx, size_gy), out_...  51.2 us
    unnamed x4, local copies, waits for them, and re-layouts  8.15 us
    pallas_call x1, Pallas kernels, on_device(): pl.pallas_call(local_kernel, out_shape=(jax.ShapeDtypeStruct((fields, sam...  5.92 us

profile of v1, /device:TPU:0, one launch (start us, length us, event | category | flops | bytes accessed | tf_op | source)
XLA Modules:
  0.0 65.9 jit_solution(1574753289418559417)
XLA Ops:
  0.6 1.3 %copy.11 = s32[128,8,4]{0,1,2:T(8,128)} copy(s32[128,8,4]{0,2,1:T(4,128)} %param.9) | data formatting | bytes 32768 | tf_op args[3]
  1.9 2.8 %copy.9.cot_ref = bf16[128,28,128]{2,1,0:T(8,128)(2,1)} copy(bf16[128,28,128]{2,0,1:T(8,128)(2,1)} %param.7) | data formatting | bytes 1835008 | tf_op args[1]
  4.7 5.9 %shard_map.77 = (bf16[8,128,128]{2,1,0:T(8,128)(2,1)}, bf16[7,128,128]{2,1,0:T(8,128)(2,1)}, s32[4,8,128]{2,1,0:T(8,128)}) custom-call(bf16[128,8,128]{2,1,0:T(8,128)(2,1)} %pooled_ref.1, bf16[128,28,128]{2,1,0:T(8,128)(2,1)} %copy.9.cot_ref, bf16[7,128,128]{2,1,0:T(8,128)(2,1)} %bil_ref.1, s32[4,8,128]{2,1,0:T(8,128)} %bitcast.10, s32[8,128]{1,0:T(8,128)} %bitcast.11, ...), custom_call_target="tpu_custom_call" | custom-call | tf_op jit(solution)/shard_map/pallas_call | solution.py:287
  10.6 51.2 %shard_map.78 = (f32[2048,128]{1,0:T(8,128)}, f32[8,112,128]{2,1,0:T(8,128)}) custom-call(bf16[8,128,128]{2,1,0:T(8,128)(2,1)} %get-tuple-element.7.grad_ref, s32[4,8,128]{2,1,0:T(8,128)} %get-tuple-element.8.ids_ref, bf16[8,112,128]{2,1,0:T(8,128)(2,1)} %bitcast.9), custom_call_target="tpu_custom_call" | custom-call | tf_op jit(solution)/shard_map/pallas_call | solution.py:307
  61.8 1.8 %copy.14 = f32[7,128,128]{2,1,0:T(8,128)} copy(f32[7,128,128]{2,1,0:T(8,128)} %bitcast.8) | data formatting | bytes 917504
  63.6 2.3 %copy.15 = f32[256,8,128]{2,1,0:T(8,128)} copy(f32[256,8,128]{2,1,0:T(8,128)} %bitcast.7) | data formatting | bytes 2097152

commit v2 on v1

v2 whole, which is shorter than its diff:
```python
import functools

import jax
import jax.numpy as jnp
from jax import lax
from jax.experimental import pallas as pl
from jax.experimental.pallas import tpu as pltpu
from jax.sharding import PartitionSpec as P

MESH = pl.DeviceIdType.MESH
BF = jnp.bfloat16
F32 = jnp.float32
LANES = 128


def pair_list(fields):
    return [(i, j) for i in range(fields) for j in range(i + 1, fields)]


def kernel(
    size_gx, size_gy,
    pooled_ref, cot_ref, bil_ref, bag_ref, lens_ref, home_ref,
    out_ref, wout_ref,
    pool_f, proj_f, meta,
    gath0, gath1, part0, part1, got0, got1,
    w0, w1, w2, w2s, w3, w3s,
    zus, zds, zr, as_, ar, ss, sr, ps, pr,
    w1s_sem, w1r_sem, w2s_sem, w2r_sem, w3s_sem, w3r_sem,
):
    samples, fields, width = pooled_ref.shape
    bag = bag_ref.shape[1]
    rows = part0.shape[2]
    piece = w0.shape[1]
    nz, ny = size_gx // 2, size_gy // 2
    plane = 2 * size_gy
    most = max(2, ny)
    gx, gy = lax.axis_index("gx"), lax.axis_index("gy")
    z, x, y, c = gx // 2, gx % 2, gy // 2, gy % 2
    seat = x * size_gy + gy
    sibling = (gx, y * 2 + 1 - c)
    gath, part, got = (gath0, gath1), (part0, part1), (got0, got1)
    wide, deep = (2, ny), (ny, 2)

    def along_x(o):
        return (z * 2 + (x + o) % 2, gy)

    def along_y(o):
        return (gx, ((y + o) % ny) * 2 + c)

    near, far = (along_x, along_y), (along_y, along_x)

    def z_peer(d):
        return (((z + d) % nz) * 2 + x, gy)

    def seat_peer(d):
        to = (seat + d) % plane
        return (z * 2 + to // size_gy, to % size_gy)

    def remote(src, dst, send, recv, dev):
        return pltpu.make_async_remote_copy(
            src_ref=src, dst_ref=dst, send_sem=send, recv_sem=recv,
            device_id=dev, device_id_type=MESH,
        )

    def z_up(g, m, s):
        slot, i = gath[m].at[g, 0, 0, s], (2 * g + m) * nz + s
        return remote(slot, slot, zus.at[i], zr.at[i], z_peer(1))

    def z_down(g, m, s):
        slot, i = gath[m].at[g, 0, 0, s], (2 * g + m) * nz + s
        return remote(slot, slot, zds.at[i], zr.at[i], z_peer(nz - 1))

    def a_copy(g, m, o, s):
        i = ((2 * g + m) * most + o) * nz + s
        return remote(
            gath[m].at[g, 0, 0, s], gath[m].at[g, 0, o, s], as_.at[i], ar.at[i], near[m](o)
        )

    def s_copy(g, m, o, s):
        i = ((2 * g + m) * most + o) * nz + s
        return remote(
            gath[m].at[g, 0, o, s], gath[m].at[g, 1, o, s], ss.at[i], sr.at[i], sibling
        )

    def p_copy(g, m, o):
        i = (2 * g + m) * most + o
        return remote(part[m].at[o, g], got[m].at[o, g], ps.at[i], pr.at[i], far[m](o))

    def w1_copy(d):
        return remote(
            w0.at[(seat + d) % plane], w1.at[d], w1s_sem.at[d], w1r_sem.at[d], seat_peer(d)
        )

    def w2_copy(d, slot):
        return remote(w2s, w2.at[slot], w2s_sem.at[d], w2r_sem.at[slot], z_peer(d))

    def w3_copy(d, slot):
        return remote(w3s, w3.at[slot], w3s_sem.at[d], w3r_sem.at[slot], seat_peer(d))

    barrier = pltpu.get_barrier_semaphore()
    for d in range(1, nz):
        pl.semaphore_signal(barrier, inc=1, device_id=z_peer(d), device_id_type=MESH)
    for d in range(1, plane):
        pl.semaphore_signal(barrier, inc=1, device_id=seat_peer(d), device_id_type=MESH)

    def spread_out(b, carry):
        pool_f[pl.ds(pl.multiple_of(b * fields, fields), fields), :] = pooled_ref[b].astype(F32)
        return carry

    lax.fori_loop(0, samples, spread_out, 0, unroll=8)

    bags = [bag_ref[:, k, :] for k in range(bag)]
    high = [b // LANES for b in bags]
    low = [b % LANES for b in bags]

    def look(h, found):
        row = home_ref[:, pl.ds(pl.multiple_of(h * LANES, LANES), LANES)]
        return tuple(
            jnp.where(high[k] == h, jnp.take_along_axis(row, low[k], axis=1), found[k])
            for k in range(bag)
        )

    none = jnp.full(lens_ref.shape, 0, jnp.int32)
    found = lax.fori_loop(0, home_ref.shape[1] // LANES, look, (none,) * bag, unroll=8)
    lens = lens_ref[...]
    for k in range(bag):
        meta[:, k, :] = jnp.where(lens > k, found[k] // rows, -1).astype(F32)
        meta[:, bag + k, :] = (found[k] % rows).astype(F32)

    pool = lambda f: pool_f[pl.ds(f, samples, stride=fields), :]
    number = {pair: p for p, pair in enumerate(pair_list(fields))}
    cot = lambda i, j: cot_ref[number[i, j]].astype(F32)

    def spread(g, m, s):
        for o in range(1, wide[m]):
            a_copy(g, m, o, s).start()
        s_copy(g, m, 0, s).start()

    for i in range(fields):
        total = None
        if i < fields - 1:
            mine = pool(i).astype(BF)
            proj_f[i] = jnp.dot(mine, bil_ref[i], preferred_element_type=F32)
            upper = jnp.zeros((samples, width), F32)
            for j in range(i + 1, fields):
                upper = upper + cot(i, j) * pool(j)
            upper = upper.astype(BF)
            wide_w = lax.dot_general(
                mine, upper, (((0,), (0,)), ((), ())), preferred_element_type=F32
            ).astype(BF)
            at, end = i * width, (i + 1) * width
            while at < end:
                p, r = at // piece, at % piece
                n = min(piece - r, end - at)
                w0[p, r : r + n, :] = wide_w[at - i * width : at - i * width + n, :]
                at += n
            total = lax.dot_general(
                upper, bil_ref[i], (((1,), (1,)), ((), ())), preferred_element_type=F32
            )
        for k in range(i):
            term = cot(k, i) * proj_f[k]
            total = term if total is None else total + term
        g, m = i // 2, i % 2
        gath[m][g, 0, 0, z, :samples, :] = total.astype(BF)
        gath[m][g, 0, 0, z, samples:, :] = meta[i].astype(BF)
        if i == 0:
            pl.semaphore_wait(barrier, nz - 1 + plane - 1)

        @pl.when(z < nz - 1)
        def _():
            z_up(g, m, z).start()

        @pl.when(z > 0)
        def _():
            z_down(g, m, z).start()

        spread(g, m, z)

    for d in range(1, plane):
        w1_copy(d).start()

    def z_stage(g, m):
        for t in range(1, nz):
            @pl.when(z - t >= 0)
            def _():
                z_up(g, m, z - t).wait_recv()

                @pl.when(z < nz - 1)
                def _():
                    z_up(g, m, z - t).start()

                spread(g, m, z - t)

            @pl.when(z + t < nz)
            def _():
                z_down(g, m, z + t).wait_recv()

                @pl.when(z > 0)
                def _():
                    z_down(g, m, z + t).start()

                spread(g, m, z + t)

    def a_stage(g, m):
        for o in range(1, wide[m]):
            for s in range(nz):
                a_copy(g, m, o, s).wait_recv()
                s_copy(g, m, o, s).start()

    def s_wait(g, m):
        for o in range(wide[m]):
            for s in range(nz):
                s_copy(g, m, o, s).wait_recv()

    row_number = lax.broadcasted_iota(jnp.int32, (rows, samples), 0).astype(F32).astype(BF)
    one, zero = jnp.ones((), BF), jnp.zeros((), BF)

    def sums_for(g, m, o):
        gx_to, gy_to = far[m](o)
        owner = (gx_to * size_gy + gy_to).astype(F32)
        blocks, values = [], []
        for core in range(2):
            for a in range(wide[m]):
                for s in range(nz):
                    note = gath[m][g, core, a, s, samples:, :].astype(F32)
                    key = jnp.where(note[:bag] == owner, note[bag:], -1.0).astype(BF)
                    count = None
                    for k in range(bag):
                        hit = jnp.where(row_number == key[k : k + 1, :], one, zero)
                        count = hit if count is None else count + hit
                    blocks.append(count)
                    values.append(gath[m][g, core, a, s, :samples, :])
        return jnp.dot(
            jnp.concatenate(blocks, axis=1),
            jnp.concatenate(values, axis=0),
            preferred_element_type=F32,
        )

    def weights_in_plane():
        total = w0[seat].astype(F32)
        for d in range(1, plane):
            w1_copy(d).wait_recv()
            total = total + w1[d].astype(F32)
        w2s[...] = total
        w2[z] = total
        for d in range(1, nz):
            w2_copy(d, z).start()

    def weights_along_z():
        for d in range(1, nz):
            w2_copy(d, (z + d) % nz).wait_recv()
        total = w2[0]
        for s in range(1, nz):
            total = total + w2[s]
        w3s[...] = total.astype(BF)
        w3[seat] = total.astype(BF)
        for d in range(1, plane):
            w3_copy(d, seat).start()

    def ahead(stage, g, m):
        if m == 0:
            stage(g, 1)
        else:
            @pl.when(g + 1 < fields // 2)
            def _():
                stage(g + 1, 0)

    z_stage(0, 0)
    a_stage(0, 0)

    def two_fields(g, carry):
        for m in range(2):
            ahead(z_stage, g, m)
            s_wait(g, m)

            def one_target(o, inner):
                part[m][o, g] = sums_for(g, m, o).astype(BF)
                p_copy(g, m, o).start()
                return inner

            lax.fori_loop(1, deep[m], one_target, 0)
            ahead(a_stage, g, m)
            out_ref[pl.ds(2 * g + m, rows, stride=fields), :] = sums_for(g, m, 0)

        @pl.when(g == 0)
        def _():
            weights_in_plane()

        @pl.when(g == 1)
        def _():
            weights_along_z()

        return carry

    lax.fori_loop(0, fields // 2, two_fields, 0)

    for d in range(1, plane):
        w3_copy(d, (seat + d) % plane).wait_recv()
    wout_ref[...] = w3[...].astype(F32)

    def finish(g, carry):
        for m in range(2):
            at = pl.ds(2 * g + m, rows, stride=fields)
            total = out_ref[at, :]
            for o in range(1, deep[m]):
                p_copy(g, m, o).wait_recv()
                total = total + got[m][o, g].astype(F32)
            out_ref[at, :] = total
        return carry

    lax.fori_loop(0, fields // 2, finish, 0)

    def drain(g, carry):
        for m in range(2):
            for s in range(nz):
                @pl.when((z >= s) & (z < nz - 1))
                def _():
                    z_up(g, m, s).wait_send()

                @pl.when((z <= s) & (z > 0))
                def _():
                    z_down(g, m, s).wait_send()

                for o in range(wide[m]):
                    if o:
                        a_copy(g, m, o, s).wait_send()
                    s_copy(g, m, o, s).wait_send()
            for o in range(1, deep[m]):
                p_copy(g, m, o).wait_send()
        return carry

    lax.fori_loop(0, fields // 2, drain, 0)
    for d in range(1, nz):
        w2_copy(d, z).wait_send()
    for d in range(1, plane):
        w1_copy(d).wait_send()
        w3_copy(d, seat).wait_send()


def on_device(size_gx, size_gy, pooled, cotangent, bilinear, bag_ids, bag_lens, row_home):
    samples, fields, width = pooled.shape
    bag = bag_ids.shape[2]
    rows = row_home.shape[1] // (size_gx * size_gy)
    nz, ny, plane = size_gx // 2, size_gy // 2, 2 * size_gy
    most, half = max(2, ny), fields // 2
    piece = (fields - 1) * width // plane
    vmem = pl.BlockSpec(memory_space=pltpu.VMEM)
    dma = pltpu.SemaphoreType.DMA
    table, weight = pl.pallas_call(
        functools.partial(kernel, size_gx, size_gy),
        out_shape=(
            jax.ShapeDtypeStruct((rows * fields, width), F32),
            jax.ShapeDtypeStruct((plane, piece, width), F32),
        ),
        in_specs=[vmem] * 6,
        out_specs=(vmem,) * 2,
        scratch_shapes=[
            pltpu.VMEM((samples * fields, width), F32),
            pltpu.VMEM((fields - 1, samples, width), F32),
            pltpu.VMEM((fields, 2 * bag, samples), F32),
            pltpu.VMEM((half, 2, 2, nz, samples + 2 * bag, width), BF),
            pltpu.VMEM((half, 2, ny, nz, samples + 2 * bag, width), BF),
            pltpu.VMEM((ny, half, rows, width), BF),
            pltpu.VMEM((2, half, rows, width), BF),
            pltpu.VMEM((ny, half, rows, width), BF),
            pltpu.VMEM((2, half, rows, width), BF),
            pltpu.VMEM((plane, piece, width), BF),
            pltpu.VMEM((plane, piece, width), BF),
            pltpu.VMEM((nz, piece, width), F32),
            pltpu.VMEM((piece, width), F32),
            pltpu.VMEM((plane, piece, width), BF),
            pltpu.VMEM((piece, width), BF),
            dma((fields * nz,)),
            dma((fields * nz,)),
            dma((fields * nz,)),
            dma((fields * most * nz,)),
            dma((fields * most * nz,)),
            dma((fields * most * nz,)),
            dma((fields * most * nz,)),
            dma((fields * most,)),
            dma((fields * most,)),
            dma((plane,)),
            dma((plane,)),
            dma((nz,)),
            dma((nz,)),
            dma((plane,)),
            dma((plane,)),
        ],
        compiler_params=pltpu.CompilerParams(collective_id=0, has_side_effects=True),
    )(
        pooled, cotangent.transpose(1, 0, 2), bilinear,
        bag_ids.transpose(1, 2, 0), bag_lens.transpose(1, 0), row_home,
    )
    return (
        weight.reshape(fields - 1, width, width),
        table.reshape(rows, fields, width),
    )


def solution(mesh):
    placed = (
        P(("gx", "gy"), None, None),
        P(("gx", "gy"), None, None),
        P(),
        P(("gx", "gy"), None, None),
        P(("gx", "gy"), None),
        P(),
    )
    return jax.shard_map(
        functools.partial(on_device, mesh.shape["gx"], mesh.shape["gy"]),
        mesh=mesh,
        in_specs=placed,
        out_specs=(P(), P(("gx", "gy"), None, None)),
        check_vma=False,
    )
```

time: 66.2 us -> 81.9 us (1.24)
  Pallas kernels: 57.1 us -> 77 us
  local copies, waits for them, and re-layouts: 8.15 us -> 4.08 us
    pallas_call x2 -> x1, Pallas kernels: 57.1 us -> 77 us  [on_device(): pl.pallas_call(functools.partial(kernel, size_gx, size_gy), out_shape=(ja...]
    unnamed x4 -> x2, local copies, waits for them, and re-layouts: 8.15 us -> 4.08 us
where the time goes in v2:
time: 81.9 us; the launch traced here: 81.7 us
  Pallas kernels  77 us (94%)
  local copies, waits for them, and re-layouts  4.08 us (5%)
    pallas_call x1, Pallas kernels, on_device(): pl.pallas_call(functools.partial(kernel, size_gx, size_gy), out_shape=(ja...  77 us
    unnamed x2, local copies, waits for them, and re-layouts  4.08 us

profile of v2, /device:TPU:0, one launch (start us, length us, event | category | flops | bytes accessed | tf_op | source)
XLA Modules:
  0.0 81.7 jit_solution(1148430316279337833)
XLA Ops:
  0.6 77.0 %shard_map.77 = (f32[2048,128]{1,0:T(8,128)}, f32[8,112,128]{2,1,0:T(8,128)}) custom-call(bf16[128,8,128]{2,1,0:T(8,128)(2,1)} %pooled_ref.1, bf16[28,128,128]{2,1,0:T(8,128)(2,1)} %bitcast.6, bf16[7,128,128]{2,1,0:T(8,128)(2,1)} %bil_ref.1, s32[8,4,128]{2,1,0:T(4,128)} %bitcast.8, s32[8,128]{1,0:T(8,128)} %bitcast.9, s32[8,8192]{1,0:T(8,128)} %home_ref.1), custom_call_target="tpu_custom_call" | custom-call | tf_op jit(solution)/shard_map/pallas_call | solution.py:349
  77.6 1.8 %copy.10 = f32[7,128,128]{2,1,0:T(8,128)} copy(f32[7,128,128]{2,1,0:T(8,128)} %bitcast.7) | data formatting | bytes 917504
  79.4 2.3 %copy.11 = f32[256,8,128]{2,1,0:T(8,128)} copy(f32[256,8,128]{2,1,0:T(8,128)} %bitcast.5) | data formatting | bytes 2097152

commit v3 on v2

v3 whole, which is shorter than its diff:
```python
import functools

import jax
import jax.numpy as jnp
from jax import lax
from jax.experimental import pallas as pl
from jax.experimental.pallas import tpu as pltpu
from jax.sharding import PartitionSpec as P

MESH = pl.DeviceIdType.MESH
BF = jnp.bfloat16
F32 = jnp.float32
LANES = 128


def pair_list(fields):
    return [(i, j) for i in range(fields) for j in range(i + 1, fields)]


def kernel(
    size_gx, size_gy,
    pooled_ref, cot_ref, bil_ref, bag_ref, lens_ref, home_ref,
    out_ref, wout_ref,
    pool_f, proj_f, meta,
    gath, part, got,
    w0, w1, w2, w2s, w3, w3s,
    zs, zr, ss, sr, ps, pr,
    w1s_sem, w1r_sem, w2s_sem, w2r_sem, w3s_sem, w3r_sem,
):
    samples, fields, width = pooled_ref.shape
    bag = bag_ref.shape[1]
    rows = part.shape[2]
    piece = w0.shape[1]
    nz, ny = size_gx // 2, size_gy // 2
    plane = 2 * size_gy
    npc = 2 * ny
    gx, gy = lax.axis_index("gx"), lax.axis_index("gy")
    z, x, y, c = gx // 2, gx % 2, gy // 2, gy % 2
    spot = x * ny + y
    seat = x * size_gy + gy
    sibling = (gx, y * 2 + 1 - c)

    def spot_peer(d):
        to = (spot + d) % npc
        return (z * 2 + to // ny, (to % ny) * 2 + c)

    def z_peer(d):
        return (((z + d) % nz) * 2 + x, gy)

    def seat_peer(d):
        to = (seat + d) % plane
        return (z * 2 + to // size_gy, to % size_gy)

    def remote(src, dst, send, recv, dev):
        return pltpu.make_async_remote_copy(
            src_ref=src, dst_ref=dst, send_sem=send, recv_sem=recv,
            device_id=dev, device_id_type=MESH,
        )

    def z_copy(f, d):
        i = f * nz + d
        return remote(gath.at[f, 0, 0], gath.at[f, 0, d], zs.at[i], zr.at[i], z_peer(d))

    def s_copy(f, d):
        i = f * nz + d
        return remote(gath.at[f, 0, d], gath.at[f, 1, d], ss.at[i], sr.at[i], sibling)

    def p_copy(f, d):
        i = f * npc + d
        return remote(part.at[d, f], got.at[d, f], ps.at[i], pr.at[i], spot_peer(d))

    def w1_copy(d):
        return remote(
            w0.at[(seat + d) % plane], w1.at[d], w1s_sem.at[d], w1r_sem.at[d], seat_peer(d)
        )

    def w2_copy(d, slot):
        return remote(w2s, w2.at[slot], w2s_sem.at[d], w2r_sem.at[slot], z_peer(d))

    def w3_copy(d, slot):
        return remote(w3s, w3.at[slot], w3s_sem.at[d], w3r_sem.at[slot], seat_peer(d))

    barrier = pltpu.get_barrier_semaphore()
    for d in range(1, nz):
        pl.semaphore_signal(barrier, inc=1, device_id=z_peer(d), device_id_type=MESH)
    for d in range(1, plane):
        pl.semaphore_signal(barrier, inc=1, device_id=seat_peer(d), device_id_type=MESH)

    def spread_out(b, carry):
        pool_f[pl.ds(pl.multiple_of(b * fields, fields), fields), :] = pooled_ref[b].astype(F32)
        return carry

    lax.fori_loop(0, samples, spread_out, 0, unroll=8)

    bags = [bag_ref[:, k, :] for k in range(bag)]
    high = [b // LANES for b in bags]
    low = [b % LANES for b in bags]

    def look(h, found):
        row = home_ref[:, pl.ds(pl.multiple_of(h * LANES, LANES), LANES)]
        return tuple(
            jnp.where(high[k] == h, jnp.take_along_axis(row, low[k], axis=1), found[k])
            for k in range(bag)
        )

    none = jnp.full(lens_ref.shape, 0, jnp.int32)
    found = lax.fori_loop(0, home_ref.shape[1] // LANES, look, (none,) * bag, unroll=8)
    lens = lens_ref[...]
    for k in range(bag):
        meta[:, k, :] = jnp.where(lens > k, found[k] // rows, -1).astype(F32)
        meta[:, bag + k, :] = (found[k] % rows).astype(F32)

    pool = lambda f: pool_f[pl.ds(f, samples, stride=fields), :]
    number = {pair: p for p, pair in enumerate(pair_list(fields))}
    cot = lambda i, j: cot_ref[number[i, j]].astype(F32)

    for i in range(fields):
        total = None
        if i < fields - 1:
            mine = pool(i).astype(BF)
            proj_f[i] = jnp.dot(mine, bil_ref[i], preferred_element_type=F32)
            upper = jnp.zeros((samples, width), F32)
            for j in range(i + 1, fields):
                upper = upper + cot(i, j) * pool(j)
            upper = upper.astype(BF)
            wide_w = lax.dot_general(
                mine, upper, (((0,), (0,)), ((), ())), preferred_element_type=F32
            ).astype(BF)
            at, end = i * width, (i + 1) * width
            while at < end:
                p, r = at // piece, at % piece
                n = min(piece - r, end - at)
                w0[p, r : r + n, :] = wide_w[at - i * width : at - i * width + n, :]
                at += n
            total = lax.dot_general(
                upper, bil_ref[i], (((1,), (1,)), ((), ())), preferred_element_type=F32
            )
        for k in range(i):
            term = cot(k, i) * proj_f[k]
            total = term if total is None else total + term
        gath[i, 0, 0, :samples, :] = total.astype(BF)
        gath[i, 0, 0, samples:, :] = meta[i].astype(BF)
        if i == 0:
            pl.semaphore_wait(barrier, nz - 1 + plane - 1)

        for d in range(1, nz):
            z_copy(i, d).start()
        s_copy(i, 0).start()

    for d in range(1, plane):
        w1_copy(d).start()

    def forward(f):
        for d in range(1, nz):
            z_copy(f, d).wait_recv()
            s_copy(f, d).start()

    row_number = lax.broadcasted_iota(jnp.int32, (rows, samples), 0).astype(F32).astype(BF)
    one, zero = jnp.ones((), BF), jnp.zeros((), BF)

    def sums_for(f, d):
        gx_to, gy_to = spot_peer(d)
        owner = (gx_to * size_gy + gy_to).astype(F32)
        blocks, values = [], []
        for core in range(2):
            for s in range(nz):
                note = gath[f, core, s, samples:, :].astype(F32)
                key = jnp.where(note[:bag] == owner, note[bag:], -1.0).astype(BF)
                count = None
                for k in range(bag):
                    hit = jnp.where(row_number == key[k : k + 1, :], one, zero)
                    count = hit if count is None else count + hit
                blocks.append(count)
                values.append(gath[f, core, s, :samples, :])
        return jnp.dot(
            jnp.concatenate(blocks, axis=1),
            jnp.concatenate(values, axis=0),
            preferred_element_type=F32,
        )

    def weights_in_plane():
        total = w0[seat].astype(F32)
        for d in range(1, plane):
            w1_copy(d).wait_recv()
            total = total + w1[d].astype(F32)
        w2s[...] = total
        w2[z] = total
        for d in range(1, nz):
            w2_copy(d, z).start()

    def weights_along_z():
        for d in range(1, nz):
            w2_copy(d, (z + d) % nz).wait_recv()
        total = w2[0]
        for s in range(1, nz):
            total = total + w2[s]
        w3s[...] = total.astype(BF)
        w3[seat] = total.astype(BF)
        for d in range(1, plane):
            w3_copy(d, seat).start()

    forward(0)

    def one_field(f, carry):
        @pl.when(f + 1 < fields)
        def _():
            forward(f + 1)

        for d in range(nz):
            s_copy(f, d).wait_recv()

        def one_target(d, inner):
            part[d, f] = sums_for(f, d).astype(BF)
            p_copy(f, d).start()
            return inner

        lax.fori_loop(1, npc, one_target, 0)
        out_ref[pl.ds(f, rows, stride=fields), :] = sums_for(f, 0)

        @pl.when(f == 1)
        def _():
            weights_in_plane()

        @pl.when(f == 3)
        def _():
            weights_along_z()

        return carry

    lax.fori_loop(0, fields, one_field, 0)

    for d in range(1, plane):
        w3_copy(d, (seat + d) % plane).wait_recv()
    wout_ref[...] = w3[...].astype(F32)

    def finish(f, carry):
        at = pl.ds(f, rows, stride=fields)
        total = out_ref[at, :]
        for d in range(1, npc):
            p_copy(f, d).wait_recv()
            total = total + got[d, f].astype(F32)
        out_ref[at, :] = total
        return carry

    lax.fori_loop(0, fields, finish, 0)

    def drain(f, carry):
        for d in range(1, nz):
            z_copy(f, d).wait_send()
        for d in range(nz):
            s_copy(f, d).wait_send()
        for d in range(1, npc):
            p_copy(f, d).wait_send()
        return carry

    lax.fori_loop(0, fields, drain, 0)
    for d in range(1, nz):
        w2_copy(d, z).wait_send()
    for d in range(1, plane):
        w1_copy(d).wait_send()
        w3_copy(d, seat).wait_send()


def on_device(size_gx, size_gy, pooled, cotangent, bilinear, bag_ids, bag_lens, row_home):
    samples, fields, width = pooled.shape
    bag = bag_ids.shape[2]
    rows = row_home.shape[1] // (size_gx * size_gy)
    nz, ny, plane = size_gx // 2, size_gy // 2, 2 * size_gy
    npc = 2 * ny
    piece = (fields - 1) * width // plane
    vmem = pl.BlockSpec(memory_space=pltpu.VMEM)
    dma = pltpu.SemaphoreType.DMA
    table, weight = pl.pallas_call(
        functools.partial(kernel, size_gx, size_gy),
        out_shape=(
            jax.ShapeDtypeStruct((rows * fields, width), F32),
            jax.ShapeDtypeStruct((plane, piece, width), F32),
        ),
        in_specs=[vmem] * 6,
        out_specs=(vmem,) * 2,
        scratch_shapes=[
            pltpu.VMEM((samples * fields, width), F32),
            pltpu.VMEM((fields - 1, samples, width), F32),
            pltpu.VMEM((fields, 2 * bag, samples), F32),
            pltpu.VMEM((fields, 2, nz, samples + 2 * bag, width), BF),
            pltpu.VMEM((npc, fields, rows, width), BF),
            pltpu.VMEM((npc, fields, rows, width), BF),
            pltpu.VMEM((plane, piece, width), BF),
            pltpu.VMEM((plane, piece, width), BF),
            pltpu.VMEM((nz, piece, width), F32),
            pltpu.VMEM((piece, width), F32),
            pltpu.VMEM((plane, piece, width), BF),
            pltpu.VMEM((piece, width), BF),
            dma((fields * nz,)),
            dma((fields * nz,)),
            dma((fields * nz,)),
            dma((fields * nz,)),
            dma((fields * npc,)),
            dma((fields * npc,)),
            dma((plane,)),
            dma((plane,)),
            dma((nz,)),
            dma((nz,)),
            dma((plane,)),
            dma((plane,)),
        ],
        compiler_params=pltpu.CompilerParams(collective_id=0, has_side_effects=True),
    )(
        pooled, cotangent.transpose(1, 0, 2), bilinear,
        bag_ids.transpose(1, 2, 0), bag_lens.transpose(1, 0), row_home,
    )
    return (
        weight.reshape(fields - 1, width, width),
        table.reshape(rows, fields, width),
    )


def solution(mesh):
    placed = (
        P(("gx", "gy"), None, None),
        P(("gx", "gy"), None, None),
        P(),
        P(("gx", "gy"), None, None),
        P(("gx", "gy"), None),
        P(),
    )
    return jax.shard_map(
        functools.partial(on_device, mesh.shape["gx"], mesh.shape["gy"]),
        mesh=mesh,
        in_specs=placed,
        out_specs=(P(), P(("gx", "gy"), None, None)),
        check_vma=False,
    )
```

time: 81.9 us -> 59.4 us (0.73)
  Pallas kernels: 77 us -> 54.4 us
    pallas_call x1, Pallas kernels: 77 us -> 54.4 us  [on_device(): pl.pallas_call(functools.partial(kernel, size_gx, size_gy), out_shape=(ja...]
where the time goes in v3:
time: 59.4 us; the launch traced here: 59.1 us
  Pallas kernels  54.4 us (92%)
  local copies, waits for them, and re-layouts  4.08 us (7%)
  between operations  0.64 us (1%)
    pallas_call x1, Pallas kernels, on_device(): pl.pallas_call(functools.partial(kernel, size_gx, size_gy), out_shape=(ja...  54.4 us
    unnamed x2, local copies, waits for them, and re-layouts  4.08 us

profile of v3, /device:TPU:0, one launch (start us, length us, event | category | flops | bytes accessed | tf_op | source)
XLA Modules:
  0.0 59.1 jit_solution(9261402214941111325)
XLA Ops:
  0.6 54.4 %shard_map.77 = (f32[2048,128]{1,0:T(8,128)}, f32[8,112,128]{2,1,0:T(8,128)}) custom-call(bf16[128,8,128]{2,1,0:T(8,128)(2,1)} %pooled_ref.1, bf16[28,128,128]{2,1,0:T(8,128)(2,1)} %bitcast.6, bf16[7,128,128]{2,1,0:T(8,128)(2,1)} %bil_ref.1, s32[8,4,128]{2,1,0:T(4,128)} %bitcast.8, s32[8,128]{1,0:T(8,128)} %bitcast.9, s32[8,8192]{1,0:T(8,128)} %home_ref.1), custom_call_target="tpu_custom_call" | custom-call | tf_op jit(solution)/shard_map/pallas_call | solution.py:273
  55.1 1.8 %copy.10 = f32[7,128,128]{2,1,0:T(8,128)} copy(f32[7,128,128]{2,1,0:T(8,128)} %bitcast.7) | data formatting | bytes 917504
  56.9 2.3 %copy.11 = f32[256,8,128]{2,1,0:T(8,128)} copy(f32[256,8,128]{2,1,0:T(8,128)} %bitcast.5) | data formatting | bytes 2097152
